TPU v7x, 32 devices: a whole 2x2x4 slice. The times are simulated.
32 devices in a mesh: nodes: 16 (over z, y, x), feat: 2 (over core).
Axes of the slice: x: 2, y: 2, z: 4, core: 2. Of those that a mesh axis runs over, the one named last changes fastest.
Arguments:
- features: bfloat16 [8192, 128], P('nodes'), may hold values from -6 to 6
- row_counts: int32 [16], P('nodes'), may hold values from 128 to 512, as said below
- send_rows: int32 [16, 16, 64], P('nodes'), may hold values from 0 to 511, as said below
- edge_src: int32 [2, 65536], P(None, 'nodes'), may hold values from 0 to 1535, as said below
- edge_dst: int32 [2, 65536], P(None, 'nodes'), may hold values from 0 to 511, as said below
- edge_keep: int32 [2, 65536], P(None, 'nodes'), may hold values 0 or 1
- w_first: bfloat16 [128, 512], P(None, 'feat'), may hold values from -0.5 to 0.5
- b_first: float32 [512], P('feat'), may hold values from -3 to 3
- w_second: bfloat16 [512, 512], P(None, 'feat'), may hold values from -0.25 to 0.25
Outputs:
- normed: bfloat16 [2, 8192, 512], P(None, 'nodes', 'feat')
- correlation: float32 [512, 512], P('nodes', 'feat')
- barlow_loss: float32 [], replicated
Inputs may be any that keep to these rules, and one draw needn't show every extreme that they name: `row_counts`: some partition has all 512 rows live. send_rows[i, j, h] is below row_counts[i]. `edge_src`: A source below 512 is below row_counts of the edge's partition. `edge_dst`: A partition's edge slots come in aligned blocks of 1024 slots; block k targets rows k * 128 to (k + 1) * 128 - 1.
All inputs are finite; a program needn't handle non-finite values. No bound on the sum of `edge_keep` on one device may be relied on, other than what follows from the above.
Results may differ from a plain program's by a relative error of at most 0.0017.
The roundings to bfloat16 on the way count: a program that leaves them out, or rounds other values in their place, can miss the bound.
Values may be sent and summed in bfloat16 or wider, within the bound.
A program may use at most 64 MiB of HBM per device.

v0:
```python
import jax
import jax.numpy as jnp
from jax import lax
from jax.sharding import PartitionSpec as P


def per_device(
    features, row_counts, send_rows, edge_src, edge_dst, edge_keep, w_first, b_first, w_second
):
    local_rows = features.shape[0]
    partitions = lax.axis_size("nodes")
    halo_rows = send_rows.shape[2]
    edge_total = edge_src.shape[1]
    tile_rows = min(128, local_rows)
    tiles = local_rows // tile_rows
    per_tile = edge_total // tiles
    live_rows = (jnp.arange(local_rows) < row_counts[0]).astype(jnp.float32)[:, None]
    kept_edges = edge_keep.astype(jnp.float32)
    outbound = send_rows[0]
    tile_base = (jnp.arange(tiles, dtype=jnp.int32) * tile_rows)[:, None]
    row_slots = jnp.arange(tile_rows, dtype=jnp.int32)
    tables = []
    degrees = []
    for view_index in range(2):
        inside = edge_dst[view_index].reshape(tiles, per_tile) - tile_base
        table = (inside[:, :, None] == row_slots[None, None, :]).astype(jnp.float32) * kept_edges[
            view_index
        ].reshape(tiles, per_tile)[:, :, None]
        tables.append(table)
        degrees.append(jnp.sum(table, 1).reshape(local_rows))

    def mix_view(lookup, view_index):
        width = lookup.shape[1]
        picked = lookup[edge_src[view_index]].astype(jnp.float32).reshape(tiles, per_tile, width)
        summed = jnp.einsum(
            "tes,tec->tsc",
            tables[view_index],
            picked,
            precision=lax.Precision.HIGHEST,
            preferred_element_type=jnp.float32,
        )
        summed = summed.reshape(local_rows, width)
        return (lookup[:local_rows].astype(jnp.float32) + summed) / (1.0 + degrees[view_index])[
            :, None
        ]

    proj = jnp.dot(features, w_first, preferred_element_type=jnp.float32)
    arrived = lax.all_to_all(proj[outbound], "nodes", split_axis=0, concat_axis=0, tiled=True)
    lookup = jnp.concatenate([proj, arrived.reshape(partitions * halo_rows, -1)], 0)
    averaged = [mix_view(lookup, view_index) for view_index in range(2)]
    hidden = jnp.stack([jax.nn.relu(branch + b_first) for branch in averaged]).astype(jnp.bfloat16)
    summed_second = jnp.einsum(
        "gnq,qm->gnm",
        lax.all_gather(hidden, "feat", axis=2, tiled=True),
        w_second,
        preferred_element_type=jnp.float32,
    )
    projected = summed_second.astype(jnp.bfloat16)
    arrived_second = lax.all_to_all(
        projected[:, outbound], "nodes", split_axis=1, concat_axis=1, tiled=True
    )
    embedded = jnp.stack(
        [
            mix_view(
                jnp.concatenate(
                    [
                        projected[view_index],
                        arrived_second[view_index].reshape(partitions * halo_rows, -1),
                    ],
                    0,
                ),
                view_index,
            )
            for view_index in range(2)
        ]
    )
    column_sums, squares, node_total = lax.psum(
        (
            jnp.sum(embedded * live_rows, 1),
            jnp.sum(jnp.square(embedded) * live_rows, 1),
            row_counts[0].astype(jnp.float32),
        ),
        "nodes",
    )
    average = column_sums / node_total
    variance = squares / node_total - jnp.square(average)
    normed = (
        (embedded - average[:, None, :]) / jnp.sqrt(variance + 1e-05)[:, None, :] * live_rows
    ).astype(jnp.bfloat16)
    wide_first = lax.all_gather(normed[0], "feat", axis=1, tiled=True)
    row_share = wide_first.shape[1] // partitions
    contract_rows = (((0,), (0,)), ((), ()))
    owned_rows = lax.psum_scatter(
        lax.dot_general(wide_first, normed[1], contract_rows, preferred_element_type=jnp.float32),
        "nodes",
        scatter_dimension=0,
        tiled=True,
    )
    correlation = owned_rows / node_total
    own_columns = correlation.shape[1]
    row_labels = (
        lax.axis_index("nodes") * row_share + jnp.arange(row_share, dtype=jnp.int32)[:, None]
    )
    column_labels = (
        lax.axis_index("feat") * own_columns + jnp.arange(own_columns, dtype=jnp.int32)[None, :]
    )
    partial_loss = jnp.sum(
        jnp.where(
            row_labels == column_labels,
            jnp.square(1.0 - correlation),
            0.005 * jnp.square(correlation),
        )
    )
    barlow_loss = lax.psum(partial_loss, ("nodes", "feat"))
    return (normed, correlation, barlow_loss)


def solution(mesh):
    placed = (
        P("nodes", None),
        P("nodes"),
        P("nodes", None, None),
        P(None, "nodes"),
        P(None, "nodes"),
        P(None, "nodes"),
        P(None, "feat"),
        P("feat"),
        P(None, "feat"),
    )
    return jax.shard_map(
        per_device,
        mesh=mesh,
        in_specs=placed,
        out_specs=(P(None, "nodes", "feat"), P("nodes", "feat"), P()),
        check_vma=False,
    )
```

profile of v0, /device:TPU:0, one launch (start us, length us, event | category | flops | bytes accessed | tf_op | source)
XLA Modules:
  0.0 345.6 jit_solution(212631927383567024)
XLA Ops:
  7.2 0.0 copy-start
  7.2 0.7 compare_select_fusion.2
  7.9 0.1 reshape.222
  8.0 1.1 fusion.39
  9.1 4.7 %gather_fusion = f32[1024,256]{1,0:T(8,128)} fusion(f32[512,256]{1,0:T(8,128)S(1)} %fusion.39, s32[1024]{0:T(1024)S(1)} %broadcast_clamp_fusion.2), kind=kCustom, calls=%fused_computation | custom fusion | bytes 2101248 | tf_op jit(solution)/shard_map/gather | solution.py:48
  13.8 8.5 %all-to-all-start = ((f32[16,64,256]{2,1,0:T(8,128)}), f32[16,64,256]{2,1,0:T(8,128)S(1)}, u32[]{:S(2)}, u32[]{:S(2)}) async-start(f32[16,64,256]{2,1,0:T(8,128)} %bitcast.1), calls=%async_computation | async-start | bytes 2097152 | tf_op jit(solution)/shard_map/all_to_all | solution.py:48
  22.3 0.0 all-gather.3.cloned.1.call-start
  22.4 0.1 slice_reduce_fusion.3
  22.5 0.1 slice_reduce_fusion.1
  22.6 0.1 broadcast_subtract_fusion.1
  22.7 0.5 select_reduce_fusion
  23.3 0.0 copy-done.4
  23.4 23.3 %all-to-all-done = f32[16,64,256]{2,1,0:T(8,128)S(1)} async-done(((f32[16,64,256]{2,1,0:T(8,128)}), f32[16,64,256]{2,1,0:T(8,128)S(1)}, u32[]{:S(2)}, u32[]{:S(2)}) %all-to-all-start) | async-done | bytes 1048608 | tf_op jit(solution)/shard_map/all_to_all | solution.py:48
  46.7 0.1 pad_maximum_fusion
  46.8 16.1 %gather_fusion.2 = f32[4096,256]{1,0:T(8,128)} fusion(f32[1536,256]{1,0:T(8,128)S(1)} %pad_maximum_fusion, s32[4096]{0:T(1024)S(1)} %broadcast_clamp_fusion), kind=kCustom, calls=%fused_computation.2 | custom fusion | bytes 8404992 | tf_op jit(solution)/shard_map/gather | solution.py:34
  62.9 5.0 %fusion.2 = f32[4,128,256]{2,1,0:T(8,128)S(1)} fusion(f32[4,1024,256]{2,1,0:T(8,128)} %bitcast.85, f32[4,1024]{1,0:T(4,128)S(1)} %mul.65, s32[4,1024]{1,0:T(4,128)S(1)} %get-tuple-element.27), kind=kOutput, calls=%fused_computation.9 | convolution fusion | flops 1611661312 | bytes 4751360 | tf_op jit(solution)/shard_map/tes,tec->tsc/dot_general | solution.py:35
  67.8 16.1 %gather_fusion.1 = f32[4096,256]{1,0:T(8,128)} fusion(f32[1536,256]{1,0:T(8,128)S(1)} %pad_maximum_fusion, s32[4096]{0:T(1024)S(1)} %broadcast_clamp_fusion.1), kind=kCustom, calls=%fused_computation.1 | custom fusion | bytes 8404992 | tf_op jit(solution)/shard_map/gather | solution.py:34
  83.9 5.0 %fusion.6 = f32[4,128,256]{2,1,0:T(8,128)S(1)} fusion(f32[4,1024,256]{2,1,0:T(8,128)} %bitcast.84, f32[4,1024]{1,0:T(4,128)S(1)} %mul.62, s32[4,1024]{1,0:T(4,128)S(1)} %get-tuple-element.26), kind=kOutput, calls=%fused_computation.14 | convolution fusion | flops 1611661312 | bytes 4751360 | tf_op jit(solution)/shard_map/tes,tec->tsc/dot_general | solution.py:35
  88.9 0.3 fusion.30
  89.2 0.8 pad_maximum_fusion.4
  90.0 0.0 all-gather.3.cloned.1.call-update
  90.0 9.2 %all-gather.3.cloned.1.call-done = bf16[2,512,512]{2,1,0:T(8,128)(2,1)} async-done(((bf16[2,512,256]{2,1,0:T(8,128)(2,1)}), bf16[2,512,512]{2,1,0:T(8,128)(2,1)}) %all-gather.3.cloned.1.call-update) | async-done | bytes 1048592 | tf_op jit(solution)/shard_map/all_gather | solution.py:54
  99.3 1.7 convolution_convert_fusion
  100.9 0.5 copy.15
  101.5 4.2 %gather_fusion.3 = bf16[1024,2,256]{2,1,0:T(2,128)(2,1)S(1)} fusion(bf16[2,512,256]{2,0,1:T(2,128)(2,1)S(1)} %copy.15, s32[1024]{0:T(1024)S(1)} %broadcast_clamp_fusion.2), kind=kCustom, calls=%fused_computation.3 | custom fusion | bytes 2101248 | tf_op jit(solution)/shard_map/gather | solution.py:60
  105.6 1.2 copy.22
  106.8 6.8 %all-to-all-start.1 = ((bf16[2,16,64,256]{3,2,0,1:T(8,128)(2,1)}), bf16[2,16,64,256]{3,2,0,1:T(8,128)(2,1)S(1)}, u32[]{:S(2)}, u32[]{:S(2)}) async-start(bf16[2,16,64,256]{3,2,0,1:T(8,128)(2,1)} %bitcast.80), calls=%async_computation.1 | async-start | bytes 2097152 | tf_op jit(solution)/shard_map/all_to_all | solution.py:59
  113.7 0.2 reduce-scatter.2.cloned.1.call-start
  114.6 23.7 %all-to-all-done.1 = bf16[2,16,64,256]{3,2,0,1:T(8,128)(2,1)S(1)} async-done(((bf16[2,16,64,256]{3,2,0,1:T(8,128)(2,1)}), bf16[2,16,64,256]{3,2,0,1:T(8,128)(2,1)S(1)}, u32[]{:S(2)}, u32[]{:S(2)}) %all-to-all-start.1) | async-done | bytes 1048608 | tf_op jit(solution)/shard_map/all_to_all | solution.py:59
  138.3 0.1 fusion.38
  138.4 0.1 pad_maximum_fusion.3
  138.5 16.9 %gather_fusion.5 = bf16[4096,256]{1,0:T(8,128)(2,1)} fusion(bf16[1536,256]{1,0:T(8,128)(2,1)S(1)} %pad_maximum_fusion.3, s32[4096]{0:T(1024)S(1)} %broadcast_clamp_fusion), kind=kCustom, calls=%fused_computation.5 | custom fusion | bytes 4210688 | tf_op jit(solution)/shard_map/gather | solution.py:34
  155.4 2.8 fusion
  158.2 0.1 pad_maximum_fusion.2
  158.3 16.9 %gather_fusion.4 = bf16[4096,256]{1,0:T(8,128)(2,1)} fusion(bf16[1536,256]{1,0:T(8,128)(2,1)S(1)} %pad_maximum_fusion.2, s32[4096]{0:T(1024)S(1)} %broadcast_clamp_fusion.1), kind=kCustom, calls=%fused_computation.4 | custom fusion | bytes 4210688 | tf_op jit(solution)/shard_map/gather | solution.py:34
  175.2 2.8 fusion.4
  178.1 0.2 fusion.23
  178.3 0.2 multiply_reduce_fusion
  178.6 42.7 %all-reduce = (f32[2,256]{1,0:T(2,128)S(1)}, f32[]{:T(128)}, f32[2,256]{1,0:T(2,128)S(1)}) all-reduce(f32[2,256]{1,0:T(2,128)S(1)} %get-tuple-element.4, f32[]{:T(128)S(6)} %convert_element_type.37, f32[2,256]{1,0:T(2,128)S(1)} %get-tuple-element.3), channel_id=1, replica_groups=mesh['nodes'=16,'feat'=2] {'nodes'}, use_global_device_ids=true, to_apply=%region_3.4 | all-reduce | flops 1025 | bytes 8200 | tf_op jit(solution)/shard_map/psum | solution.py:77
  221.3 0.7 add_sqrt_fusion
  222.0 0.2 multiply_convert_fusion
  222.1 0.0 copy-start.1
  222.2 2.2 all-gather
  224.3 1.1 fusion.20
  225.5 0.0 reduce-scatter.2.cloned.1.call-update
  225.5 73.4 %reduce-scatter.2.cloned.1.call-done = f32[32,256]{1,0:T(8,128)} async-done(((f32[512,256]{1,0:T(8,128)}), f32[32,256]{1,0:T(8,128)}) %reduce-scatter.2.cloned.1.call-update) | async-done | bytes 32784 | tf_op jit(solution)/shard_map/reduce_scatter | solution.py:93
  299.0 2.7 select_reduce_fusion.2
  301.7 37.0 %psum.31 = f32[]{:T(128)} all-reduce(f32[]{:T(128)} %get-tuple-element.12), channel_id=1, replica_groups=mesh['nodes'=16,'feat'=2] {'nodes','feat'}, use_global_device_ids=true, to_apply=%region_9.10 | all-reduce | flops 1 | bytes 8 | tf_op jit(solution)/shard_map/psum | solution.py:114
  (26 shorter events, 0.2 us)
Async XLA Ops:
  7.2 92.1 %copy-start = (bf16[512,256]{1,0:T(8,128)(2,1)S(1)}, bf16[512,256]{1,0:T(8,128)(2,1)}, u32[]{:S(2)}) copy-start(bf16[512,256]{1,0:T(8,128)(2,1)} %param.17) | copy-start | bytes 786436
  13.8 8.5 %copy-start.2 = (s32[2,4096]{1,0:T(2,128)S(1)}, s32[2,4096]{1,0:T(2,128)}, u32[]{:S(2)}) copy-start(s32[2,4096]{1,0:T(2,128)} %param.13) | copy-start | bytes 98308
  13.8 8.7 %copy-start.3 = (s32[2,4096]{1,0:T(2,128)S(1)}, s32[2,4096]{1,0:T(2,128)}, u32[]{:S(2)}) copy-start(s32[2,4096]{1,0:T(2,128)} %param.14) | copy-start | bytes 98308
  13.8 9.5 %copy-start.4 = (s32[2,4096]{1,0:T(2,128)S(1)}, s32[2,4096]{1,0:T(2,128)}, u32[]{:S(2)}) copy-start(s32[2,4096]{1,0:T(2,128)} %param.12) | copy-start | bytes 98308
  13.8 32.9 %all-to-all-start = ((f32[16,64,256]{2,1,0:T(8,128)}), f32[16,64,256]{2,1,0:T(8,128)S(1)}, u32[]{:S(2)}, u32[]{:S(2)}) async-start(f32[16,64,256]{2,1,0:T(8,128)} %bitcast.1), calls=%async_computation | async-start | bytes 2097152 | tf_op jit(solution)/shard_map/all_to_all | solution.py:48
  22.3 77.0 %all-gather.3.cloned.1.call-start = ((), (), s32[]{:S(2)}) async-start(), calls=%async_computation.3 | async-start | bytes 1572864 | tf_op jit(solution)/shard_map/all_gather | solution.py:54
  83.9 5.0 %copy-start.5 = (f32[256]{0:T(256)S(1)}, f32[256]{0:T(256)}, u32[]{:S(2)}) copy-start(f32[256]{0:T(256)} %param.16) | copy-start | bytes 3076
  106.8 31.5 %all-to-all-start.1 = ((bf16[2,16,64,256]{3,2,0,1:T(8,128)(2,1)}), bf16[2,16,64,256]{3,2,0,1:T(8,128)(2,1)S(1)}, u32[]{:S(2)}, u32[]{:S(2)}) async-start(bf16[2,16,64,256]{3,2,0,1:T(8,128)(2,1)} %bitcast.80), calls=%async_computation.1 | async-start | bytes 2097152 | tf_op jit(solution)/shard_map/all_to_all | solution.py:59
  113.7 185.3 %reduce-scatter.2.cloned.1.call-start = ((), (), s32[]{:S(2)}) async-start(), calls=%async_computation.4 | async-start | bytes 557056 | tf_op jit(solution)/shard_map/reduce_scatter | solution.py:93
  222.1 116.6 %copy-start.1 = (bf16[2,512,256]{2,1,0:T(8,128)(2,1)}, bf16[2,512,256]{2,1,0:T(8,128)(2,1)S(1)}, u32[]{:S(2)}) copy-start(bf16[2,512,256]{2,1,0:T(8,128)(2,1)S(1)} %multiply_convert_fusion) | copy-start | bytes 1572868
Sparse Core Ops, SparseCore 0:
  90.2 9.0 all-gather.2
  225.6 73.2 reduce-scatter.1
where the time goes:
time: 347 us; the launch traced here: 346 us
  waiting for transfers between devices  130 us (37%)
  blocking collectives  82 us (24%)
  local copies, waits for them, and re-layouts  77 us (22%)
  matrix products  19.5 us (6%)
  starting transfers between devices  15.6 us (4%)
  between operations  15 us (4%)
  other arithmetic  6.75 us (2%)
    reduce_scatter x1, waiting for transfers between devices, per_device(): lax.psum_scatter(lax.dot_general(wide_first, normed[1], contract_rows, pr...  73.4 us
    gather x4, local copies, waits for them, and re-layouts, mix_view(): lookup[edge_src[view_index]].astype(jnp.float32)  66 us
    psum x1, blocking collectives, per_device(): lax.psum((jnp.sum(embedded * live_rows, 1), jnp.sum(jnp.square(embedded)...  42.7 us
    psum x1, blocking collectives, per_device(): barlow_loss = lax.psum(partial_loss, ('nodes', 'feat'))  37 us
    all_to_all x1, waiting for transfers between devices, per_device(): lax.all_to_all(projected[:, outbound], 'nodes', split_axis=1, concat_axis...  23.7 us
    all_to_all x1, waiting for transfers between devices, per_device(): lax.all_to_all(proj[outbound], 'nodes', split_axis=0, concat_axis=0, tile...  23.3 us
    dot_general x4, matrix products, mix_view(): jnp.einsum('tes,tec->tsc', tables[view_index], picked, precision=lax.Prec...  15.6 us
    all_gather x1, waiting for transfers between devices, per_device(): lax.all_gather(hidden, 'feat', axis=2, tiled=True)  9.21 us
  transfers between devices with their start and end apart: 4, of which 4 were waited for; matrix products, arithmetic and copies ran while one was open for 0% of the time, Pallas kernels for 0%

commit v1 on v0

v1 whole, which is shorter than its diff:
```python
import functools

import jax
import jax.numpy as jnp
from jax import lax
from jax.experimental import pallas as pl
from jax.experimental.pallas import tpu as pltpu
from jax.sharding import PartitionSpec as P

MESH = pl.DeviceIdType.MESH
F32 = jnp.float32
BF16 = jnp.bfloat16
TILE = 128


def dot(a, b):
    return jnp.dot(a, b, preferred_element_type=F32)


def kernel(
    parts, feats,
    feat_ref, count_ref, send_ref, src_ref, dst_ref, keep_ref, wf_ref, bf_ref, ws_ref,
    normed_ref, corr_ref, loss_ref,
    pad, pick, gath1, tab1, gath2, tab2, a_hi, a_lo, deg, wf_all, bf_all, ws_all, hid, acc,
    st_own, st_all, mine, other, p_send, p_recv, l_own, l_all,
    send_sem, recv_sem, w_send, w_recv, n_send, n_recv,
):
    me = lax.axis_index("nodes")
    core = lax.axis_index("feat")
    mate = 1 - core
    rows, width = feat_ref.shape
    halo = send_ref.shape[2]
    emb = hid.shape[1]
    half = ws_ref.shape[1]
    tiles = rows // TILE
    per_tile = src_ref.shape[1] // tiles
    sources = tab1.shape[0]
    share = p_send.shape[1]
    others = parts - 1

    def peer(offset):
        return lax.rem(me + offset, parts)

    def each(fn):
        def body(offset, carry):
            fn(peer(offset))
            return carry
        lax.fori_loop(1, parts, body, 0)

    barrier = pltpu.get_barrier_semaphore()

    def greet(offset, carry):
        to = peer(offset)
        pl.semaphore_signal(barrier, inc=1, device_id={"nodes": to, "feat": core}, device_id_type=MESH)
        pl.semaphore_signal(barrier, inc=1, device_id={"nodes": to, "feat": mate}, device_id_type=MESH)
        return carry

    lax.fori_loop(1, parts, greet, 0)
    pl.semaphore_signal(barrier, inc=1, device_id={"nodes": me, "feat": mate}, device_id_type=MESH)

    pad[...] = jnp.zeros_like(pad)
    pad[0:parts, 0:halo] = send_ref[0].astype(F32)
    turned = pad[...].T
    lanes = lax.broadcasted_iota(jnp.int32, (halo, rows), 1).astype(F32)
    for p in range(parts):
        hot = turned[0:halo, p:p + 1] == lanes
        pick[p * halo:(p + 1) * halo, :] = jnp.where(hot, 1.0, 0.0).astype(BF16)
    tab1[0:rows, :] = feat_ref[...]
    out_rows = parts * halo
    step_rows = min(512, out_rows)

    def gather(table, dst):
        def body(c, carry):
            at = pl.ds(pl.multiple_of(c * step_rows, step_rows), step_rows)
            dst[at, :] = dot(pick[at, :], table()).astype(BF16)
            return carry
        lax.fori_loop(0, out_rows // step_rows, body, 0)

    gather(lambda: feat_ref[...], gath1)

    pl.semaphore_wait(barrier, parts * feats - 1)

    def slot(p):
        return pl.ds(pl.multiple_of(p * halo, halo), halo)

    def landing(p):
        return pl.ds(pl.multiple_of(rows + p * halo, halo), halo)

    def remote(src, dst, ssem, rsem, to, c):
        return pltpu.make_async_remote_copy(
            src_ref=src, dst_ref=dst, send_sem=ssem, recv_sem=rsem,
            device_id={"nodes": to, "feat": c}, device_id_type=MESH,
        )

    def drain(ref, sem):
        pltpu.make_async_copy(ref, ref, sem).wait()

    each(lambda to: remote(
        gath1.at[slot(to)], tab1.at[landing(me)], send_sem.at[0], recv_sem.at[0], to, core).start())
    weights = [
        remote(wf_ref, wf_all.at[core], w_send.at[0], w_recv.at[0], me, mate),
        remote(bf_ref, bf_all.at[core], w_send.at[1], w_recv.at[1], me, mate),
        remote(ws_ref, ws_all.at[core], w_send.at[2], w_recv.at[2], me, mate),
    ]
    for copy in weights:
        copy.start()
    wf_all[core] = wf_ref[...]
    bf_all[core] = bf_ref[...]
    ws_all[core] = ws_ref[...]
    tab1[landing(me), :] = gath1[slot(me), :]

    chunk = 256
    first_view = core == 0

    def view_row(ref, k):
        at = pl.ds(pl.multiple_of(k * per_tile, per_tile), per_tile)
        return jnp.where(first_view, ref[0:1, at], ref[1:2, at])

    def count_tile(k, carry):
        src = view_row(src_ref, k)
        dst = jnp.where(view_row(keep_ref, k) == 1, view_row(dst_ref, k) - k * TILE, -1)
        row_at = lax.broadcasted_iota(jnp.int32, (TILE, per_tile), 0)
        hits = jnp.where(row_at == dst, 1.0, 0.0)
        at = pl.ds(pl.multiple_of(k * TILE, TILE), TILE)
        deg[at, :] = 1.0 / (1.0 + jnp.sum(hits, axis=1, keepdims=True))
        hits = hits.astype(BF16)

        def count_chunk(c, inner):
            source_at = lax.broadcasted_iota(jnp.int32, (chunk, per_tile), 0)
            hot = jnp.where(source_at == src - c * chunk, 1.0, 0.0).astype(BF16)
            counts = lax.dot_general(hits, hot, (((1,), (1,)), ((), ())), preferred_element_type=F32)
            self_row = lax.broadcasted_iota(jnp.int32, (TILE, chunk), 0) + k * TILE
            self_col = lax.broadcasted_iota(jnp.int32, (TILE, chunk), 1) + c * chunk
            counts = counts + jnp.where(self_row == self_col, 1.0, 0.0)
            high = counts.astype(BF16)
            cols = pl.ds(pl.multiple_of(c * chunk, chunk), chunk)
            a_hi[at, cols] = high
            a_lo[at, cols] = (counts - high.astype(F32)).astype(BF16)
            return inner

        lax.fori_loop(0, sources // chunk, count_chunk, 0)
        return carry

    lax.fori_loop(0, tiles, count_tile, 0)

    depth = 512 if sources % 512 == 0 else 256

    def mixed(table, c):
        cols = pl.ds(pl.multiple_of(c * depth, depth), depth)
        part = table[cols, :]
        return dot(a_hi[:, cols], part) + dot(a_lo[:, cols], part)

    drain(tab1.at[pl.ds(rows, others * halo)], recv_sem.at[0])
    summed = lax.fori_loop(
        0, sources // depth, lambda c, total: total + mixed(tab1, c), jnp.zeros((rows, width), F32))
    part0 = summed.astype(BF16)
    rest = summed - part0.astype(F32)
    part1 = rest.astype(BF16)
    part2 = (rest - part1.astype(F32)).astype(BF16)
    for copy in weights:
        copy.wait_recv()
    for h in range(feats):
        w = wf_all[h]
        proj = dot(part0, w) + (dot(part1, w) + dot(part2, w))
        hid[:, h * half:(h + 1) * half] = jnp.maximum(proj * deg[...] + bf_all[h], 0.0).astype(BF16)
    for h in range(feats):
        tab2[0:rows, h * half:(h + 1) * half] = dot(hid[...], ws_all[h]).astype(BF16)

    gather(lambda: tab2[0:rows, :], gath2)
    each(lambda to: remote(
        gath2.at[slot(to)], tab2.at[landing(me)], send_sem.at[1], recv_sem.at[1], to, core).start())
    tab2[landing(me), :] = gath2[slot(me), :]
    local = rows // depth
    acc[...] = mixed(tab2, 0)
    for c in range(1, local):
        acc[...] += mixed(tab2, c)
    drain(tab2.at[pl.ds(rows, others * halo)], recv_sem.at[1])

    def add_chunk(c, carry):
        acc[...] += mixed(tab2, c)
        return carry

    lax.fori_loop(local, sources // depth, add_chunk, 0)

    live_count = count_ref[0]
    live = lax.broadcasted_iota(jnp.int32, (rows, 1), 0) < live_count
    mine_count = live_count.astype(F32)
    blocks = emb // TILE
    for q in range(blocks):
        cols = slice(q * TILE, (q + 1) * TILE)
        value = acc[:, cols] * deg[...]
        acc[:, cols] = value
        total = jnp.sum(jnp.where(live, value, 0.0), axis=0, keepdims=True)
        off = jnp.where(live, value - total / mine_count, 0.0)
        st_own[q:q + 1, :] = total
        st_own[blocks + q:blocks + q + 1, :] = jnp.sum(off * off, axis=0, keepdims=True)
    tail = st_own.shape[0] - 2 * blocks
    st_own[2 * blocks:, :] = jnp.zeros((tail, TILE), F32) + mine_count
    each(lambda to: remote(
        st_own, st_all.at[me], send_sem.at[2], recv_sem.at[2], to, core).start())
    st_all[me] = st_own[...]
    drain(st_all.at[pl.ds(0, others)], recv_sem.at[2])
    sizes = st_all[:, 2 * blocks:2 * blocks + 1, :]
    sums = st_all[:, 0:blocks, :]
    spreads = st_all[:, blocks:2 * blocks, :]
    node_total = jnp.sum(sizes, axis=0)
    average = jnp.sum(sums, axis=0) / node_total
    shift = sums / sizes - average[None]
    variance = jnp.sum(spreads + sizes * shift * shift, axis=0) / node_total
    scale = 1.0 / jnp.sqrt(variance + 1e-05)
    for q in range(blocks):
        value = (acc[:, q * TILE:(q + 1) * TILE] - average[q:q + 1, :]) * scale[q:q + 1, :]
        per_half = half // TILE
        at = (q % per_half) * TILE
        mine[q // per_half, :, at:at + TILE] = jnp.where(live, value, 0.0).astype(BF16)

    swap = remote(mine.at[mate], other.at[mate], n_send.at[0], n_recv.at[0], me, mate)
    extra = remote(mine.at[core], other.at[core], n_send.at[1], n_recv.at[1], me, mate)
    swap.start()

    @pl.when(first_view)
    def _():
        extra.start()

    normed_ref[core] = mine[core]
    contract = (((0,), (0,)), ((), ()))

    def put(h, product):
        per = half // share
        for j in range(per):
            p_send[h * per + j] = product[j * share:(j + 1) * share, :]

    swap.wait_recv()
    normed_ref[mate] = other[core]

    @pl.when(first_view)
    def _():
        for h in range(feats):
            put(h, lax.dot_general(mine[h], other[0], contract, preferred_element_type=F32))

    @pl.when(jnp.logical_not(first_view))
    def _():
        put(1, lax.dot_general(other[1], mine[1], contract, preferred_element_type=F32))
        pltpu.make_async_copy(other.at[0], other.at[0], n_recv.at[1]).wait()
        put(0, lax.dot_general(other[0], mine[1], contract, preferred_element_type=F32))

    each(lambda to: remote(
        p_send.at[to], p_recv.at[me], send_sem.at[3], recv_sem.at[3], to, core).start())
    p_recv[me] = p_send[me]
    drain(p_recv.at[pl.ds(0, others)], recv_sem.at[3])
    total = node_total[:, 0:1]
    corr = jnp.sum(p_recv[...], axis=0) / total
    corr_ref[...] = corr
    row_label = lax.broadcasted_iota(jnp.int32, (share, half), 0) + me * share
    col_label = lax.broadcasted_iota(jnp.int32, (share, half), 1) + core * half
    miss = 1.0 - corr
    terms = jnp.where(row_label == col_label, miss * miss, 0.005 * (corr * corr))
    line = jnp.sum(terms, axis=0, keepdims=True)
    folded = line[:, 0:TILE]
    for q in range(1, half // TILE):
        folded = folded + line[:, q * TILE:(q + 1) * TILE]
    l_own[...] = folded
    spot = me * feats + core

    def tell(offset, carry):
        to = peer(offset)
        remote(l_own, l_all.at[spot], send_sem.at[4], recv_sem.at[4], to, core).start()
        remote(l_own, l_all.at[spot], send_sem.at[4], recv_sem.at[4], to, mate).start()
        return carry

    lax.fori_loop(1, parts, tell, 0)
    remote(l_own, l_all.at[spot], send_sem.at[4], recv_sem.at[4], me, mate).start()
    l_all[spot] = folded
    drain(l_all.at[pl.ds(0, parts * feats - 1)], recv_sem.at[4])
    loss_ref[0, 0] = jnp.sum(l_all[...])

    for copy in weights:
        copy.wait_send()
    swap.wait_send()

    @pl.when(first_view)
    def _():
        extra.wait_send()

    drain(gath1.at[pl.ds(0, others * halo)], send_sem.at[0])
    drain(gath2.at[pl.ds(0, others * halo)], send_sem.at[1])
    drain(st_all.at[pl.ds(0, others)], send_sem.at[2])
    drain(p_send.at[pl.ds(0, others)], send_sem.at[3])
    drain(l_all.at[pl.ds(0, parts * feats - 1)], send_sem.at[4])


def per_device(
    features, row_counts, send_rows, edge_src, edge_dst, edge_keep, w_first, b_first, w_second
):
    parts = lax.axis_size("nodes")
    feats = lax.axis_size("feat")
    rows, width = features.shape
    halo = send_rows.shape[2]
    half = w_first.shape[1]
    hidden, emb_half = w_second.shape
    emb = emb_half * feats
    share = emb // parts
    sources = rows + parts * halo
    blocks = emb // TILE
    vmem = pl.BlockSpec(memory_space=pltpu.VMEM)
    smem = pl.BlockSpec(memory_space=pltpu.SMEM)
    pad_rows = -(-parts // TILE) * TILE
    normed, correlation, loss = pl.pallas_call(
        functools.partial(kernel, parts, feats),
        out_shape=(
            jax.ShapeDtypeStruct((2, rows, emb_half), BF16),
            jax.ShapeDtypeStruct((share, emb_half), F32),
            jax.ShapeDtypeStruct((1, 1), F32),
        ),
        in_specs=[vmem, smem] + [vmem] * 7,
        out_specs=(vmem, vmem, smem),
        scratch_shapes=[
            pltpu.VMEM((pad_rows, TILE), F32),
            pltpu.VMEM((parts * halo, rows), BF16),
            pltpu.VMEM((parts * halo, width), BF16),
            pltpu.VMEM((sources, width), BF16),
            pltpu.VMEM((parts * halo, emb), BF16),
            pltpu.VMEM((sources, emb), BF16),
            pltpu.VMEM((rows, sources), BF16),
            pltpu.VMEM((rows, sources), BF16),
            pltpu.VMEM((rows, 1), F32),
            pltpu.VMEM((feats, width, half), BF16),
            pltpu.VMEM((feats, 1, half), F32),
            pltpu.VMEM((feats, hidden, emb_half), BF16),
            pltpu.VMEM((rows, hidden), BF16),
            pltpu.VMEM((rows, emb), F32),
            pltpu.VMEM((2 * blocks + 8, TILE), F32),
            pltpu.VMEM((parts, 2 * blocks + 8, TILE), F32),
            pltpu.VMEM((feats, rows, emb_half), BF16),
            pltpu.VMEM((feats, rows, emb_half), BF16),
            pltpu.VMEM((parts, share, emb_half), F32),
            pltpu.VMEM((parts, share, emb_half), F32),
            pltpu.VMEM((1, TILE), F32),
            pltpu.VMEM((parts * feats, 1, TILE), F32),
            pltpu.SemaphoreType.DMA((5,)),
            pltpu.SemaphoreType.DMA((5,)),
            pltpu.SemaphoreType.DMA((3,)),
            pltpu.SemaphoreType.DMA((3,)),
            pltpu.SemaphoreType.DMA((2,)),
            pltpu.SemaphoreType.DMA((2,)),
        ],
        compiler_params=pltpu.CompilerParams(
            collective_id=0, has_side_effects=True, vmem_limit_bytes=60 * 1024 * 1024
        ),
    )(
        features, row_counts, send_rows, edge_src, edge_dst, edge_keep, w_first,
        b_first.reshape(1, half), w_second,
    )
    return normed, correlation, loss.reshape(())


def solution(mesh):
    placed = (
        P("nodes", None),
        P("nodes"),
        P("nodes", None, None),
        P(None, "nodes"),
        P(None, "nodes"),
        P(None, "nodes"),
        P(None, "feat"),
        P("feat"),
        P(None, "feat"),
    )
    return jax.shard_map(
        per_device,
        mesh=mesh,
        in_specs=placed,
        out_specs=(P(None, "nodes", "feat"), P("nodes", "feat"), P()),
        check_vma=False,
    )
```

time: 347 us -> 79.8 us (0.23)
  waiting for transfers between devices: 130 us -> 0 us
  blocking collectives: 82 us -> 0 us
  local copies, waits for them, and re-layouts: 77 us -> 2.49 us
  Pallas kernels: 0 us -> 74.2 us
  matrix products: 19.5 us -> 0 us
  starting transfers between devices: 15.6 us -> 0 us
  between operations: 15 us -> 2.98 us
  other arithmetic: 6.75 us -> 0 us
    psum x2 -> x0, blocking collectives: 79.8 us -> none  [the longest x1 42.7 us: per_device(): lax.psum((jnp.sum(embedded * live_rows, 1), jnp.sum(jnp.square(embedded)...]
    gather x7 -> x0, local copies, waits for them, and re-layouts: 76 us -> none  [the longest x4 66 us: mix_view(): lookup[edge_src[view_index]].astype(jnp.float32)]
    pallas_call x0 -> x1, Pallas kernels: none -> 74.2 us  [per_device(): pl.pallas_call(functools.partial(kernel, parts, feats), out_shape=(jax.Sh...]
    reduce_scatter x1 -> x0, waiting for transfers between devices: 73.4 us -> none  [per_device(): lax.psum_scatter(lax.dot_general(wide_first, normed[1], contract_rows, pr...]
    all_to_all x2 -> x0, waiting for transfers between devices: 47 us -> none  [the longest x1 23.7 us: per_device(): lax.all_to_all(projected[:, outbound], 'nodes', split_axis=1, concat_axis...]
    dot_general x7 -> x0, matrix products: 19.5 us -> none  [the longest x4 15.6 us: mix_view(): jnp.einsum('tes,tec->tsc', tables[view_index], picked, precision=lax.Prec...]
    all_to_all x2 -> x0, starting transfers between devices: 15.3 us -> none  [the longest x1 8.47 us: per_device(): lax.all_to_all(proj[outbound], 'nodes', split_axis=0, concat_axis=0, tile...]
    all_gather x1 -> x0, waiting for transfers between devices: 9.21 us -> none  [per_device(): lax.all_gather(hidden, 'feat', axis=2, tiled=True)]
  transfers between devices with their start and end apart: 4 -> 0, of which waited for: 4 -> 0; matrix products, arithmetic and copies ran while one was open for 0% -> 0% of each run, Pallas kernels for 0% -> 0%
where the time goes in v1:
time: 79.8 us; the launch traced here: 79.6 us
  Pallas kernels  74.2 us (93%)
  between operations  2.98 us (4%)
  local copies, waits for them, and re-layouts  2.49 us (3%)
    pallas_call x1, Pallas kernels, per_device(): pl.pallas_call(functools.partial(kernel, parts, feats), out_shape=(jax.Sh...  74.2 us
    unnamed x4, local copies, waits for them, and re-layouts  2.49 us

profile of v1, /device:TPU:0, one launch (start us, length us, event | category | flops | bytes accessed | tf_op | source)
XLA Modules:
  0.0 79.6 jit_solution(10705608252780199889)
XLA Ops:
  1.3 74.2 %shard_map.112 = (bf16[2,512,256]{2,1,0:T(8,128)(2,1)}, f32[32,256]{1,0:T(8,128)}, f32[1,1]{1,0:T(1,128)}) custom-call(bf16[512,128]{1,0:T(8,128)(2,1)} %feat_ref.1, s32[1]{0:T(128)S(6)} %copy.15.count_ref, s32[1,16,64]{2,1,0:T(8,128)} %send_ref.1, s32[2,4096]{1,0:T(2,128)} %src_ref.1, s32[2,4096]{1,0:T(2,128)} %dst_ref.1, s32[2,4096]{1,0:T(2,128)} %keep_ref.1, ...), custom_call_target="tpu_custom_call" | custom-call | tf_op jit(solution)/shard_map/pallas_call | solution.py:308
  75.4 0.0 copy-start
  75.4 1.9 %copy.16 = bf16[2,512,256]{2,1,0:T(8,128)(2,1)} copy(bf16[2,512,256]{2,1,0:T(8,128)(2,1)} %get-tuple-element.12) | data formatting | bytes 1048576
  77.3 0.0 copy-done
  77.3 0.6 copy.17
Async XLA Ops:
  75.4 1.9 %copy-start = (f32[32,256]{1,0:T(8,128)S(1)}, f32[32,256]{1,0:T(8,128)}, u32[]{:S(2)}) copy-start(f32[32,256]{1,0:T(8,128)} %get-tuple-element.13) | copy-start | bytes 98308

commit v2 on v1

--- a/solution.py
+++ b/solution.py
@@ -17,11 +17,19 @@
     return jnp.dot(a, b, preferred_element_type=F32)
 
 
+def split(value, count):
+    found = []
+    for _ in range(count - 1):
+        found.append(value.astype(BF16))
+        value = value - found[-1].astype(F32)
+    return found + [value.astype(BF16)]
+
+
 def kernel(
     parts, feats,
     feat_ref, count_ref, send_ref, src_ref, dst_ref, keep_ref, wf_ref, bf_ref, ws_ref,
     normed_ref, corr_ref, loss_ref,
-    pad, pick, gath1, tab1, gath2, tab2, a_hi, a_lo, deg, wf_all, bf_all, ws_all, hid, acc,
+    pad, pick, gath1, tab1, gath2, tabm, tab2, a_hi, a_lo, deg, wf_all, bf_all, ws_all, hid, acc,
     st_own, st_all, mine, other, p_send, p_recv, l_own, l_all,
     send_sem, recv_sem, w_send, w_recv, n_send, n_recv,
 ):
@@ -153,30 +161,44 @@
     drain(tab1.at[pl.ds(rows, others * halo)], recv_sem.at[0])
     summed = lax.fori_loop(
         0, sources // depth, lambda c, total: total + mixed(tab1, c), jnp.zeros((rows, width), F32))
-    part0 = summed.astype(BF16)
-    rest = summed - part0.astype(F32)
-    part1 = rest.astype(BF16)
-    part2 = (rest - part1.astype(F32)).astype(BF16)
+    mean = summed * deg[...]
+    tabm[0:rows, :] = mean
+    parts3 = split(mean, 3)
+
+    def gather_mean(c, carry):
+        at = pl.ds(pl.multiple_of(c * step_rows, step_rows), step_rows)
+        hot = pick[at, :]
+        gath2[at, :] = dot(hot, parts3[0]) + (dot(hot, parts3[1]) + dot(hot, parts3[2]))
+        return carry
+
+    lax.fori_loop(0, out_rows // step_rows, gather_mean, 0)
+    each(lambda to: remote(
+        gath2.at[slot(to)], tabm.at[landing(me)], send_sem.at[1], recv_sem.at[1], to, core).start())
+    tabm[landing(me), :] = gath2[slot(me), :]
     for copy in weights:
         copy.wait_recv()
-    for h in range(feats):
-        w = wf_all[h]
-        proj = dot(part0, w) + (dot(part1, w) + dot(part2, w))
-        hid[:, h * half:(h + 1) * half] = jnp.maximum(proj * deg[...] + bf_all[h], 0.0).astype(BF16)
-    for h in range(feats):
-        tab2[0:rows, h * half:(h + 1) * half] = dot(hid[...], ws_all[h]).astype(BF16)
-
-    gather(lambda: tab2[0:rows, :], gath2)
-    each(lambda to: remote(
-        gath2.at[slot(to)], tab2.at[landing(me)], send_sem.at[1], recv_sem.at[1], to, core).start())
-    tab2[landing(me), :] = gath2[slot(me), :]
+
+    def rows_of(c):
+        at = pl.ds(pl.multiple_of(c * depth, depth), depth)
+        wide = jnp.concatenate(split(tabm[at, :], 2), axis=1)
+        for h in range(feats):
+            w = wf_all[h]
+            proj = dot(wide, jnp.concatenate([w, w], axis=0))
+            hid[:, h * half:(h + 1) * half] = jnp.maximum(proj + bf_all[h], 0.0).astype(BF16)
+        for h in range(feats):
+            tab2[at, h * half:(h + 1) * half] = dot(hid[...], ws_all[h]).astype(BF16)
+
     local = rows // depth
-    acc[...] = mixed(tab2, 0)
-    for c in range(1, local):
-        acc[...] += mixed(tab2, c)
-    drain(tab2.at[pl.ds(rows, others * halo)], recv_sem.at[1])
+    for c in range(local):
+        rows_of(c)
+        if c == 0:
+            acc[...] = mixed(tab2, c)
+        else:
+            acc[...] += mixed(tab2, c)
+    drain(tabm.at[pl.ds(rows, others * halo)], recv_sem.at[1])
 
     def add_chunk(c, carry):
+        rows_of(c)
         acc[...] += mixed(tab2, c)
         return carry
 
@@ -319,7 +341,8 @@
             pltpu.VMEM((parts * halo, rows), BF16),
             pltpu.VMEM((parts * halo, width), BF16),
             pltpu.VMEM((sources, width), BF16),
-            pltpu.VMEM((parts * halo, emb), BF16),
+            pltpu.VMEM((parts * halo, width), F32),
+            pltpu.VMEM((sources, width), F32),
             pltpu.VMEM((sources, emb), BF16),
             pltpu.VMEM((rows, sources), BF16),
             pltpu.VMEM((rows, sources), BF16),
@@ -327,7 +350,7 @@
             pltpu.VMEM((feats, width, half), BF16),
             pltpu.VMEM((feats, 1, half), F32),
             pltpu.VMEM((feats, hidden, emb_half), BF16),
-            pltpu.VMEM((rows, hidden), BF16),
+            pltpu.VMEM((512 if sources % 512 == 0 else 256, hidden), BF16),
             pltpu.VMEM((rows, emb), F32),
             pltpu.VMEM((2 * blocks + 8, TILE), F32),
             pltpu.VMEM((parts, 2 * blocks + 8, TILE), F32),

time: 79.8 us -> 67.1 us (0.84)
  Pallas kernels: 74.2 us -> 61.4 us
    pallas_call x1, Pallas kernels: 74.2 us -> 61.4 us  [per_device(): pl.pallas_call(functools.partial(kernel, parts, feats), out_shape=(jax.Sh...]
where the time goes in v2:
time: 67.1 us; the launch traced here: 66.9 us
  Pallas kernels  61.4 us (92%)
  between operations  2.98 us (4%)
  local copies, waits for them, and re-layouts  2.49 us (4%)
    pallas_call x1, Pallas kernels, per_device(): pl.pallas_call(functools.partial(kernel, parts, feats), out_shape=(jax.Sh...  61.4 us
    unnamed x4, local copies, waits for them, and re-layouts  2.49 us

profile of v2, /device:TPU:0, one launch (start us, length us, event | category | flops | bytes accessed | tf_op | source)
XLA Modules:
  0.0 66.9 jit_solution(13553172393858024667)
XLA Ops:
  1.3 61.4 %shard_map.112 = (bf16[2,512,256]{2,1,0:T(8,128)(2,1)}, f32[32,256]{1,0:T(8,128)}, f32[1,1]{1,0:T(1,128)}) custom-call(bf16[512,128]{1,0:T(8,128)(2,1)} %feat_ref.1, s32[1]{0:T(128)S(6)} %copy.15.count_ref, s32[1,16,64]{2,1,0:T(8,128)} %send_ref.1, s32[2,4096]{1,0:T(2,128)} %src_ref.1, s32[2,4096]{1,0:T(2,128)} %dst_ref.1, s32[2,4096]{1,0:T(2,128)} %keep_ref.1, ...), custom_call_target="tpu_custom_call" | custom-call | tf_op jit(solution)/shard_map/pallas_call | solution.py:330
  62.7 0.0 copy-start
  62.7 1.9 %copy.16 = bf16[2,512,256]{2,1,0:T(8,128)(2,1)} copy(bf16[2,512,256]{2,1,0:T(8,128)(2,1)} %get-tuple-element.12) | data formatting | bytes 1048576
  64.6 0.0 copy-done
  64.6 0.6 copy.17
Async XLA Ops:
  62.7 1.9 %copy-start = (f32[32,256]{1,0:T(8,128)S(1)}, f32[32,256]{1,0:T(8,128)}, u32[]{:S(2)}) copy-start(f32[32,256]{1,0:T(8,128)} %get-tuple-element.13) | copy-start | bytes 98308

commit v3 on v2

--- a/solution.py
+++ b/solution.py
@@ -30,7 +30,7 @@
     feat_ref, count_ref, send_ref, src_ref, dst_ref, keep_ref, wf_ref, bf_ref, ws_ref,
     normed_ref, corr_ref, loss_ref,
     pad, pick, gath1, tab1, gath2, tabm, tab2, a_hi, a_lo, deg, wf_all, bf_all, ws_all, hid, acc,
-    st_own, st_all, mine, other, p_send, p_recv, l_own, l_all,
+    st_own, st_all, mine, other, p_send, p_recv, l_own, l_mate, l_sum, l_all,
     send_sem, recv_sem, w_send, w_recv, n_send, n_recv,
 ):
     me = lax.axis_index("nodes")
@@ -282,18 +282,15 @@
     for q in range(1, half // TILE):
         folded = folded + line[:, q * TILE:(q + 1) * TILE]
     l_own[...] = folded
-    spot = me * feats + core
-
-    def tell(offset, carry):
-        to = peer(offset)
-        remote(l_own, l_all.at[spot], send_sem.at[4], recv_sem.at[4], to, core).start()
-        remote(l_own, l_all.at[spot], send_sem.at[4], recv_sem.at[4], to, mate).start()
-        return carry
-
-    lax.fori_loop(1, parts, tell, 0)
-    remote(l_own, l_all.at[spot], send_sem.at[4], recv_sem.at[4], me, mate).start()
-    l_all[spot] = folded
-    drain(l_all.at[pl.ds(0, parts * feats - 1)], recv_sem.at[4])
+    pair = remote(l_own, l_mate, n_send.at[2], n_recv.at[2], me, mate)
+    pair.start()
+    pair.wait_recv()
+    both = folded + l_mate[...]
+    l_sum[...] = both
+    each(lambda to: remote(
+        l_sum, l_all.at[me], send_sem.at[4], recv_sem.at[4], to, core).start())
+    l_all[me] = both
+    drain(l_all.at[pl.ds(0, others)], recv_sem.at[4])
     loss_ref[0, 0] = jnp.sum(l_all[...])
 
     for copy in weights:
@@ -308,7 +305,8 @@
     drain(gath2.at[pl.ds(0, others * halo)], send_sem.at[1])
     drain(st_all.at[pl.ds(0, others)], send_sem.at[2])
     drain(p_send.at[pl.ds(0, others)], send_sem.at[3])
-    drain(l_all.at[pl.ds(0, parts * feats - 1)], send_sem.at[4])
+    pair.wait_send()
+    drain(l_all.at[pl.ds(0, others)], send_sem.at[4])
 
 
 def per_device(
@@ -359,13 +357,15 @@
             pltpu.VMEM((parts, share, emb_half), F32),
             pltpu.VMEM((parts, share, emb_half), F32),
             pltpu.VMEM((1, TILE), F32),
-            pltpu.VMEM((parts * feats, 1, TILE), F32),
+            pltpu.VMEM((1, TILE), F32),
+            pltpu.VMEM((1, TILE), F32),
+            pltpu.VMEM((parts, 1, TILE), F32),
             pltpu.SemaphoreType.DMA((5,)),
             pltpu.SemaphoreType.DMA((5,)),
             pltpu.SemaphoreType.DMA((3,)),
             pltpu.SemaphoreType.DMA((3,)),
-            pltpu.SemaphoreType.DMA((2,)),
-            pltpu.SemaphoreType.DMA((2,)),
+            pltpu.SemaphoreType.DMA((3,)),
+            pltpu.SemaphoreType.DMA((3,)),
         ],
         compiler_params=pltpu.CompilerParams(
             collective_id=0, has_side_effects=True, vmem_limit_bytes=60 * 1024 * 1024

time: 67.1 us -> 68.6 us (1.022)
  Pallas kernels: 61.4 us -> 62.9 us
    pallas_call x1, Pallas kernels: 61.4 us -> 62.9 us  [per_device(): pl.pallas_call(functools.partial(kernel, parts, feats), out_shape=(jax.Sh...]
where the time goes in v3:
time: 68.6 us; the launch traced here: 68.4 us
  Pallas kernels  62.9 us (92%)
  between operations  2.98 us (4%)
  local copies, waits for them, and re-layouts  2.49 us (4%)
    pallas_call x1, Pallas kernels, per_device(): pl.pallas_call(functools.partial(kernel, parts, feats), out_shape=(jax.Sh...  62.9 us
    unnamed x4, local copies, waits for them, and re-layouts  2.49 us

profile of v3, /device:TPU:0, one launch (start us, length us, event | category | flops | bytes accessed | tf_op | source)
XLA Modules:
  0.0 68.4 jit_solution(1386353132136187770)
XLA Ops:
  1.3 62.9 %shard_map.112 = (bf16[2,512,256]{2,1,0:T(8,128)(2,1)}, f32[32,256]{1,0:T(8,128)}, f32[1,1]{1,0:T(1,128)}) custom-call(bf16[512,128]{1,0:T(8,128)(2,1)} %feat_ref.1, s32[1]{0:T(128)S(6)} %copy.15.count_ref, s32[1,16,64]{2,1,0:T(8,128)} %send_ref.1, s32[2,4096]{1,0:T(2,128)} %src_ref.1, s32[2,4096]{1,0:T(2,128)} %dst_ref.1, s32[2,4096]{1,0:T(2,128)} %keep_ref.1, ...), custom_call_target="tpu_custom_call" | custom-call | tf_op jit(solution)/shard_map/pallas_call | solution.py:328
  64.2 0.0 copy-start
  64.2 1.9 %copy.16 = bf16[2,512,256]{2,1,0:T(8,128)(2,1)} copy(bf16[2,512,256]{2,1,0:T(8,128)(2,1)} %get-tuple-element.12) | data formatting | bytes 1048576
  66.1 0.0 copy-done
  66.1 0.6 copy.17
Async XLA Ops:
  64.2 1.9 %copy-start = (f32[32,256]{1,0:T(8,128)S(1)}, f32[32,256]{1,0:T(8,128)}, u32[]{:S(2)}) copy-start(f32[32,256]{1,0:T(8,128)} %get-tuple-element.13) | copy-start | bytes 98308
